TPU v7x, 8 devices: a whole 2x2x1 slice. The times are simulated.
8 devices in a mesh: stage: 4 (over z, y, x), tp: 2 (over core).
Axes of the slice: x: 2, y: 2, z: 1, core: 2. Of those that a mesh axis runs over, the one named last changes fastest.
Arguments:
- x: bfloat16 [4, 4096, 1536], P(None, 'tp')
- g: bfloat16 [4, 2, 1536], P('stage')
- w1: bfloat16 [4, 2, 1536, 6144], P('stage', None, None, 'tp')
- w2: bfloat16 [4, 2, 6144, 1536], P('stage', None, 'tp')
Outputs:
- output: bfloat16 [4, 4, 4096, 1536], P('stage', None, 'tp')
All inputs are finite; a program needn't handle non-finite values.
Results may differ from a plain program's by a relative error of at most 0.0197235.
Values are sent between devices in bfloat16 or wider.
A program may use at most 1 GiB of HBM per device.

v0:
```python
import jax
import jax.numpy as jnp
from jax import lax
from jax.sharding import PartitionSpec as P

EPS = 1e-5


def _ln(y, g):
    yf = y.astype(jnp.float32)
    mu = jnp.mean(yf, axis=-1, keepdims=True)
    var = jnp.mean(jnp.square(yf - mu), axis=-1, keepdims=True)
    return ((yf - mu) * lax.rsqrt(var + EPS) * g.astype(jnp.float32)).astype(jnp.bfloat16)


def _block(y, g, w1, w2):
    h = lax.all_gather(_ln(y, g), 'tp', axis=0, tiled=True)
    a = jax.nn.gelu(jnp.dot(h, w1, preferred_element_type=jnp.float32)).astype(jnp.bfloat16)
    p = jnp.dot(a, w2, preferred_element_type=jnp.float32).astype(jnp.bfloat16)
    r = lax.psum_scatter(p, 'tp', scatter_dimension=0, tiled=True)
    return (y.astype(jnp.float32) + r.astype(jnp.float32)).astype(jnp.bfloat16)


def solution(mesh):
    S = mesh.shape['stage']
    fwd = [(i, i + 1) for i in range(S - 1)]

    def local(x, g, w1, w2):
        s = lax.axis_index('stage')
        M = x.shape[0]
        nb = g.shape[1]
        out = jnp.zeros_like(x)
        recv = jnp.zeros_like(x[0])
        for k in range(M + S - 1):
            y = jnp.where(s == 0, x[min(k, M - 1)], recv)
            for b in range(nb):
                y = _block(y, g[0, b], w1[0, b], w2[0, b])
            m = k - s
            mc = jnp.clip(m, 0, M - 1)
            old = lax.dynamic_index_in_dim(out, mc, 0, keepdims=False)
            out = lax.dynamic_update_index_in_dim(out, jnp.where((m >= 0) & (m < M), y, old), mc, 0)
            if k < M + S - 2:
                recv = lax.ppermute(y, 'stage', fwd)
        return out[None]

    return jax.shard_map(
        local, mesh=mesh,
        in_specs=(P(None, 'tp', None), P('stage', None, None),
                  P('stage', None, None, 'tp'), P('stage', None, 'tp', None)),
        out_specs=P('stage', None, 'tp', None), check_vma=False)
```

profile of v0, /device:TPU:7, one launch (start us, length us, event | category | flops | bytes accessed | tf_op | source)
XLA Modules:
  0.0 3182.1 jit_solution(12435988591172677597)
XLA Ops:
  49.2 55.7 %fusion.7.clone.2 = bf16[4096,3072]{1,0:T(8,128)(2,1)} fusion(bf16[4096,1536]{1,0:T(8,128)(2,1)} %all-gather.15.cloned.1.call-done, bf16[1,2,1536,3072]{3,2,1,0:T(8,128)(2,1)} %param.6), kind=kOutput, calls=%fused_computation.21.clone.clone.clone | convolution fusion | flops 38767951872 | bytes 47185920 | tf_op jit(solution)/shard_map/dot_general | solution.py:18
  206.1 55.7 %fusion.15.clone.2 = bf16[4096,3072]{1,0:T(8,128)(2,1)} fusion(bf16[4096,1536]{1,0:T(8,128)(2,1)} %all-gather.17.cloned.1.call-done, bf16[1,2,1536,3072]{3,2,1,0:T(8,128)(2,1)} %param.6), kind=kOutput, calls=%fused_computation.29.clone.clone.clone | convolution fusion | flops 38767951872 | bytes 47185920 | tf_op jit(solution)/shard_map/dot_general | solution.py:18
  347.3 137.3 %collective-permute-done = bf16[2048,1536]{1,0:T(8,128)(2,1)S(1)} collective-permute-done((bf16[2048,1536]{1,0:T(8,128)(2,1)}, bf16[2048,1536]{1,0:T(8,128)(2,1)S(1)}, u32[]{:S(2)}, u32[]{:S(2)}) %collective-permute-start) | collective-permute-done | bytes 6291488 | tf_op jit(solution)/shard_map/ppermute | solution.py:43
  521.1 55.7 %fusion.23.clone.2 = bf16[4096,3072]{1,0:T(8,128)(2,1)} fusion(bf16[4096,1536]{1,0:T(8,128)(2,1)} %all-gather.19.cloned.1.call-done, bf16[1,2,1536,3072]{3,2,1,0:T(8,128)(2,1)} %param.6), kind=kOutput, calls=%fused_computation.37.clone.clone.clone | convolution fusion | flops 38767951872 | bytes 47185920 | tf_op jit(solution)/shard_map/dot_general | solution.py:18
  576.9 46.7 %convolution_convert_fusion.11 = bf16[4096,1536]{1,0:T(8,128)(2,1)} fusion(bf16[1,2,3072,1536]{3,2,1,0:T(8,128)(2,1)} %param.7, bf16[4096,3072]{1,0:T(8,128)(2,1)} %fusion.23.clone.2), kind=kOutput, calls=%fused_computation.180 | convolution fusion | flops 38660997120 | bytes 47185920 | tf_op jit(solution)/shard_map/dot_general | solution.py:19
  686.1 55.7 %fusion.31.clone.2 = bf16[4096,3072]{1,0:T(8,128)(2,1)} fusion(bf16[4096,1536]{1,0:T(8,128)(2,1)} %all-gather.21.cloned.1.call-done, bf16[1,2,1536,3072]{3,2,1,0:T(8,128)(2,1)} %param.6), kind=kOutput, calls=%fused_computation.45.clone.clone.clone | convolution fusion | flops 38767951872 | bytes 47185920 | tf_op jit(solution)/shard_map/dot_general | solution.py:18
  741.8 46.7 %convolution_convert_fusion.10 = bf16[4096,1536]{1,0:T(8,128)(2,1)} fusion(bf16[1,2,3072,1536]{3,2,1,0:T(8,128)(2,1)} %param.7, bf16[4096,3072]{1,0:T(8,128)(2,1)} %fusion.31.clone.2), kind=kOutput, calls=%fused_computation.179 | convolution fusion | flops 38660997120 | bytes 47185920 | tf_op jit(solution)/shard_map/dot_general | solution.py:19
  818.1 137.4 %collective-permute-done.1 = bf16[2048,1536]{1,0:T(8,128)(2,1)S(1)} collective-permute-done((bf16[2048,1536]{1,0:T(8,128)(2,1)S(1)}, bf16[2048,1536]{1,0:T(8,128)(2,1)S(1)}, u32[]{:S(2)}, u32[]{:S(2)}) %collective-permute-start.1) | collective-permute-done | bytes 6291488 | tf_op jit(solution)/shard_map/ppermute | solution.py:43
  992.0 55.7 %fusion.39.clone.2 = bf16[4096,3072]{1,0:T(8,128)(2,1)} fusion(bf16[4096,1536]{1,0:T(8,128)(2,1)} %all-gather.23.cloned.1.call-done, bf16[1,2,1536,3072]{3,2,1,0:T(8,128)(2,1)} %param.6), kind=kOutput, calls=%fused_computation.53.clone.clone.clone | convolution fusion | flops 38767951872 | bytes 47185920 | tf_op jit(solution)/shard_map/dot_general | solution.py:18
  1047.7 46.7 %convolution_convert_fusion.9 = bf16[4096,1536]{1,0:T(8,128)(2,1)} fusion(bf16[1,2,3072,1536]{3,2,1,0:T(8,128)(2,1)} %param.7, bf16[4096,3072]{1,0:T(8,128)(2,1)} %fusion.39.clone.2), kind=kOutput, calls=%fused_computation.178 | convolution fusion | flops 38660997120 | bytes 47185920 | tf_op jit(solution)/shard_map/dot_general | solution.py:19
  1156.9 55.7 %fusion.47.clone.2 = bf16[4096,3072]{1,0:T(8,128)(2,1)} fusion(bf16[4096,1536]{1,0:T(8,128)(2,1)} %all-gather.25.cloned.1.call-done, bf16[1,2,1536,3072]{3,2,1,0:T(8,128)(2,1)} %param.6), kind=kOutput, calls=%fused_computation.61.clone.clone.clone | convolution fusion | flops 38767951872 | bytes 47185920 | tf_op jit(solution)/shard_map/dot_general | solution.py:18
  1212.7 46.7 %convolution_convert_fusion.8 = bf16[4096,1536]{1,0:T(8,128)(2,1)} fusion(bf16[1,2,3072,1536]{3,2,1,0:T(8,128)(2,1)} %param.7, bf16[4096,3072]{1,0:T(8,128)(2,1)} %fusion.47.clone.2), kind=kOutput, calls=%fused_computation.177 | convolution fusion | flops 38660997120 | bytes 47185920 | tf_op jit(solution)/shard_map/dot_general | solution.py:19
  1289.0 137.4 %collective-permute-done.2 = bf16[2048,1536]{1,0:T(8,128)(2,1)S(1)} collective-permute-done((bf16[2048,1536]{1,0:T(8,128)(2,1)S(1)}, bf16[2048,1536]{1,0:T(8,128)(2,1)S(1)}, u32[]{:S(2)}, u32[]{:S(2)}) %collective-permute-start.2) | collective-permute-done | bytes 6291488 | tf_op jit(solution)/shard_map/ppermute | solution.py:43
  1462.9 55.7 %fusion.55.clone.2 = bf16[4096,3072]{1,0:T(8,128)(2,1)} fusion(bf16[4096,1536]{1,0:T(8,128)(2,1)} %all-gather.27.cloned.1.call-done, bf16[1,2,1536,3072]{3,2,1,0:T(8,128)(2,1)} %param.6), kind=kOutput, calls=%fused_computation.69.clone.clone.clone | convolution fusion | flops 38767951872 | bytes 47185920 | tf_op jit(solution)/shard_map/dot_general | solution.py:18
  1518.6 46.7 %convolution_convert_fusion.7 = bf16[4096,1536]{1,0:T(8,128)(2,1)} fusion(bf16[1,2,3072,1536]{3,2,1,0:T(8,128)(2,1)} %param.7, bf16[4096,3072]{1,0:T(8,128)(2,1)} %fusion.55.clone.2), kind=kOutput, calls=%fused_computation.176 | convolution fusion | flops 38660997120 | bytes 47185920 | tf_op jit(solution)/shard_map/dot_general | solution.py:19
  1627.8 55.7 %fusion.63.clone.2 = bf16[4096,3072]{1,0:T(8,128)(2,1)} fusion(bf16[4096,1536]{1,0:T(8,128)(2,1)} %all-gather.29.cloned.1.call-done, bf16[1,2,1536,3072]{3,2,1,0:T(8,128)(2,1)} %param.6), kind=kOutput, calls=%fused_computation.77.clone.clone.clone | convolution fusion | flops 38767951872 | bytes 47185920 | tf_op jit(solution)/shard_map/dot_general | solution.py:18
  1683.5 46.7 %convolution_convert_fusion.6 = bf16[4096,1536]{1,0:T(8,128)(2,1)} fusion(bf16[1,2,3072,1536]{3,2,1,0:T(8,128)(2,1)} %param.7, bf16[4096,3072]{1,0:T(8,128)(2,1)} %fusion.63.clone.2), kind=kOutput, calls=%fused_computation.175 | convolution fusion | flops 38660997120 | bytes 47185920 | tf_op jit(solution)/shard_map/dot_general | solution.py:19
  1759.9 137.4 %collective-permute-done.3 = bf16[2048,1536]{1,0:T(8,128)(2,1)S(1)} collective-permute-done((bf16[2048,1536]{1,0:T(8,128)(2,1)S(1)}, bf16[2048,1536]{1,0:T(8,128)(2,1)S(1)}, u32[]{:S(2)}, u32[]{:S(2)}) %collective-permute-start.3) | collective-permute-done | bytes 6291488 | tf_op jit(solution)/shard_map/ppermute | solution.py:43
  1933.7 55.7 %fusion.71.clone.2 = bf16[4096,3072]{1,0:T(8,128)(2,1)} fusion(bf16[4096,1536]{1,0:T(8,128)(2,1)} %all-gather.31.cloned.1.call-done, bf16[1,2,1536,3072]{3,2,1,0:T(8,128)(2,1)} %param.6), kind=kOutput, calls=%fused_computation.85.clone.clone.clone | convolution fusion | flops 38767951872 | bytes 47185920 | tf_op jit(solution)/shard_map/dot_general | solution.py:18
  1989.4 46.7 %convolution_convert_fusion.5 = bf16[4096,1536]{1,0:T(8,128)(2,1)} fusion(bf16[1,2,3072,1536]{3,2,1,0:T(8,128)(2,1)} %param.7, bf16[4096,3072]{1,0:T(8,128)(2,1)} %fusion.71.clone.2), kind=kOutput, calls=%fused_computation.174 | convolution fusion | flops 38660997120 | bytes 47185920 | tf_op jit(solution)/shard_map/dot_general | solution.py:19
  2098.6 55.7 %fusion.79.clone.2 = bf16[4096,3072]{1,0:T(8,128)(2,1)} fusion(bf16[4096,1536]{1,0:T(8,128)(2,1)} %all-gather.33.cloned.1.call-done, bf16[1,2,1536,3072]{3,2,1,0:T(8,128)(2,1)} %param.6), kind=kOutput, calls=%fused_computation.93.clone.clone.clone | convolution fusion | flops 38767951872 | bytes 47185920 | tf_op jit(solution)/shard_map/dot_general | solution.py:18
  2154.4 46.7 %convolution_convert_fusion.4 = bf16[4096,1536]{1,0:T(8,128)(2,1)} fusion(bf16[1,2,3072,1536]{3,2,1,0:T(8,128)(2,1)} %param.7, bf16[4096,3072]{1,0:T(8,128)(2,1)} %fusion.79.clone.2), kind=kOutput, calls=%fused_computation.173 | convolution fusion | flops 38660997120 | bytes 47185920 | tf_op jit(solution)/shard_map/dot_general | solution.py:19
  2230.7 137.4 %collective-permute-done.4 = bf16[2048,1536]{1,0:T(8,128)(2,1)S(1)} collective-permute-done((bf16[2048,1536]{1,0:T(8,128)(2,1)S(1)}, bf16[2048,1536]{1,0:T(8,128)(2,1)S(1)}, u32[]{:S(2)}, u32[]{:S(2)}) %collective-permute-start.4) | collective-permute-done | bytes 6291488 | tf_op jit(solution)/shard_map/ppermute | solution.py:43
  2404.6 55.7 %fusion.87.clone.2 = bf16[4096,3072]{1,0:T(8,128)(2,1)} fusion(bf16[4096,1536]{1,0:T(8,128)(2,1)} %all-gather.35.cloned.1.call-done, bf16[1,2,1536,3072]{3,2,1,0:T(8,128)(2,1)} %param.6), kind=kOutput, calls=%fused_computation.101.clone.clone.clone | convolution fusion | flops 38767951872 | bytes 47185920 | tf_op jit(solution)/shard_map/dot_general | solution.py:18
  2460.3 46.7 %convolution_convert_fusion.3 = bf16[4096,1536]{1,0:T(8,128)(2,1)} fusion(bf16[1,2,3072,1536]{3,2,1,0:T(8,128)(2,1)} %param.7, bf16[4096,3072]{1,0:T(8,128)(2,1)} %fusion.87.clone.2), kind=kOutput, calls=%fused_computation.172 | convolution fusion | flops 38660997120 | bytes 47185920 | tf_op jit(solution)/shard_map/dot_general | solution.py:19
  2569.5 55.7 %fusion.95.clone.2 = bf16[4096,3072]{1,0:T(8,128)(2,1)} fusion(bf16[4096,1536]{1,0:T(8,128)(2,1)} %all-gather.37.cloned.1.call-done, bf16[1,2,1536,3072]{3,2,1,0:T(8,128)(2,1)} %param.6), kind=kOutput, calls=%fused_computation.109.clone.clone.clone | convolution fusion | flops 38767951872 | bytes 47185920 | tf_op jit(solution)/shard_map/dot_general | solution.py:18
  2625.3 46.7 %convolution_convert_fusion.2 = bf16[4096,1536]{1,0:T(8,128)(2,1)} fusion(bf16[1,2,3072,1536]{3,2,1,0:T(8,128)(2,1)} %param.7, bf16[4096,3072]{1,0:T(8,128)(2,1)} %fusion.95.clone.2), kind=kOutput, calls=%fused_computation.171 | convolution fusion | flops 38660997120 | bytes 47185920 | tf_op jit(solution)/shard_map/dot_general | solution.py:19
  2701.6 137.3 %collective-permute-done.5 = bf16[2048,1536]{1,0:T(8,128)(2,1)S(1)} collective-permute-done((bf16[2048,1536]{1,0:T(8,128)(2,1)S(1)}, bf16[2048,1536]{1,0:T(8,128)(2,1)S(1)}, u32[]{:S(2)}, u32[]{:S(2)}) %collective-permute-start.5) | collective-permute-done | bytes 6291488 | tf_op jit(solution)/shard_map/ppermute | solution.py:43
  2875.5 55.7 %fusion.103.clone.5 = bf16[4096,3072]{1,0:T(8,128)(2,1)} fusion(bf16[4096,1536]{1,0:T(8,128)(2,1)} %all-gather.39.cloned.1.call-done, bf16[1,2,1536,3072]{3,2,1,0:T(8,128)(2,1)} %param.6), kind=kOutput, calls=%fused_computation.117.clone.clone.clone.2 | convolution fusion | flops 38767951872 | bytes 47185920 | tf_op jit(solution)/shard_map/dot_general | solution.py:18
  2931.2 46.7 %convolution_convert_fusion.1 = bf16[4096,1536]{1,0:T(8,128)(2,1)} fusion(bf16[1,2,3072,1536]{3,2,1,0:T(8,128)(2,1)} %param.7, bf16[4096,3072]{1,0:T(8,128)(2,1)} %fusion.103.clone.5), kind=kOutput, calls=%fused_computation.170 | convolution fusion | flops 38660997120 | bytes 47185920 | tf_op jit(solution)/shard_map/dot_general | solution.py:19
  3040.4 55.7 %fusion.111.clone.5 = bf16[4096,3072]{1,0:T(8,128)(2,1)} fusion(bf16[4096,1536]{1,0:T(8,128)(2,1)} %all-gather.41.cloned.1.call-done, bf16[1,2,1536,3072]{3,2,1,0:T(8,128)(2,1)} %param.6), kind=kOutput, calls=%fused_computation.125.clone.clone.clone.2 | convolution fusion | flops 38767951872 | bytes 47185920 | tf_op jit(solution)/shard_map/dot_general | solution.py:18
  3096.1 46.7 %convolution_convert_fusion = bf16[4096,1536]{1,0:T(8,128)(2,1)} fusion(bf16[1,2,3072,1536]{3,2,1,0:T(8,128)(2,1)} %param.7, bf16[4096,3072]{1,0:T(8,128)(2,1)} %fusion.111.clone.5), kind=kOutput, calls=%fused_computation.169 | convolution fusion | flops 38660997120 | bytes 47185920 | tf_op jit(solution)/shard_map/dot_general | solution.py:19
  (221 shorter events, 1002.3 us)
Async XLA Ops:
  24.5 144.3 %reduce-scatter.15.cloned.1.call-start = ((), (), s32[]{:S(2)}) async-start(), calls=%async_computation.15 | async-start | bytes 18874368 | tf_op jit(solution)/shard_map/reduce_scatter | solution.py:20
  181.9 143.8 %reduce-scatter.17.cloned.1.call-start = ((), (), s32[]{:S(2)}) async-start(), calls=%async_computation.17 | async-start | bytes 18874368 | tf_op jit(solution)/shard_map/reduce_scatter | solution.py:20
  308.5 212.6 %all-gather.19.cloned.1.call-start = ((), (), s32[]{:S(2)}) async-start(), calls=%async_computation.18 | async-start | bytes 18874368 | tf_op jit(solution)/shard_map/all_gather | solution.py:17
  345.7 138.9 %collective-permute-start = (bf16[2048,1536]{1,0:T(8,128)(2,1)}, bf16[2048,1536]{1,0:T(8,128)(2,1)S(1)}, u32[]{:S(2)}, u32[]{:S(2)}) collective-permute-start(bf16[2048,1536]{1,0:T(8,128)(2,1)} %get-tuple-element.42), channel_id=1, source_target_pairs={{0,2},{2,4},{4,6},{1,3},{3,5},{5,7}} | collective-permute-start | bytes 18874376 | tf_op jit(solution)/shard_map/ppermute | solution.py:43
  495.9 144.9 %reduce-scatter.19.cloned.1.call-start = ((), (), s32[]{:S(2)}) async-start(), calls=%async_computation.19 | async-start | bytes 18874368 | tf_op jit(solution)/shard_map/reduce_scatter | solution.py:20
  623.6 62.4 %all-gather.21.cloned.1.call-start = ((), (), s32[]{:S(2)}) async-start(), calls=%async_computation.20 | async-start | bytes 18874368 | tf_op jit(solution)/shard_map/all_gather | solution.py:17
  661.9 143.8 %reduce-scatter.21.cloned.1.call-start = ((), (), s32[]{:S(2)}) async-start(), calls=%async_computation.21 | async-start | bytes 18874368 | tf_op jit(solution)/shard_map/reduce_scatter | solution.py:20
  788.6 203.4 %all-gather.23.cloned.1.call-start = ((), (), s32[]{:S(2)}) async-start(), calls=%async_computation.22 | async-start | bytes 18874368 | tf_op jit(solution)/shard_map/all_gather | solution.py:17
  816.5 138.9 %collective-permute-start.1 = (bf16[2048,1536]{1,0:T(8,128)(2,1)S(1)}, bf16[2048,1536]{1,0:T(8,128)(2,1)S(1)}, u32[]{:S(2)}, u32[]{:S(2)}) collective-permute-start(bf16[2048,1536]{1,0:T(8,128)(2,1)S(1)} %get-tuple-element.36), channel_id=1, source_target_pairs={{0,2},{2,4},{4,6},{1,3},{3,5},{5,7}} | collective-permute-start | bytes 18874376 | tf_op jit(solution)/shard_map/ppermute | solution.py:43
  966.8 144.9 %reduce-scatter.23.cloned.1.call-start = ((), (), s32[]{:S(2)}) async-start(), calls=%async_computation.23 | async-start | bytes 18874368 | tf_op jit(solution)/shard_map/reduce_scatter | solution.py:20
  1094.5 62.4 %all-gather.25.cloned.1.call-start = ((), (), s32[]{:S(2)}) async-start(), calls=%async_computation.24 | async-start | bytes 18874368 | tf_op jit(solution)/shard_map/all_gather | solution.py:17
  1132.8 143.8 %reduce-scatter.25.cloned.1.call-start = ((), (), s32[]{:S(2)}) async-start(), calls=%async_computation.25 | async-start | bytes 18874368 | tf_op jit(solution)/shard_map/reduce_scatter | solution.py:20
  1259.4 203.4 %all-gather.27.cloned.1.call-start = ((), (), s32[]{:S(2)}) async-start(), calls=%async_computation.26 | async-start | bytes 18874368 | tf_op jit(solution)/shard_map/all_gather | solution.py:17
  1287.4 138.9 %collective-permute-start.2 = (bf16[2048,1536]{1,0:T(8,128)(2,1)S(1)}, bf16[2048,1536]{1,0:T(8,128)(2,1)S(1)}, u32[]{:S(2)}, u32[]{:S(2)}) collective-permute-start(bf16[2048,1536]{1,0:T(8,128)(2,1)S(1)} %get-tuple-element.30), channel_id=1, source_target_pairs={{0,2},{2,4},{4,6},{1,3},{3,5},{5,7}} | collective-permute-start | bytes 18874376 | tf_op jit(solution)/shard_map/ppermute | solution.py:43
  1437.7 144.9 %reduce-scatter.27.cloned.1.call-start = ((), (), s32[]{:S(2)}) async-start(), calls=%async_computation.27 | async-start | bytes 18874368 | tf_op jit(solution)/shard_map/reduce_scatter | solution.py:20
  1565.4 62.4 %all-gather.29.cloned.1.call-start = ((), (), s32[]{:S(2)}) async-start(), calls=%async_computation.28 | async-start | bytes 18874368 | tf_op jit(solution)/shard_map/all_gather | solution.py:17
  1603.7 143.8 %reduce-scatter.29.cloned.1.call-start = ((), (), s32[]{:S(2)}) async-start(), calls=%async_computation.29 | async-start | bytes 18874368 | tf_op jit(solution)/shard_map/reduce_scatter | solution.py:20
  1730.3 203.4 %all-gather.31.cloned.1.call-start = ((), (), s32[]{:S(2)}) async-start(), calls=%async_computation.30 | async-start | bytes 18874368 | tf_op jit(solution)/shard_map/all_gather | solution.py:17
  1758.3 138.9 %collective-permute-start.3 = (bf16[2048,1536]{1,0:T(8,128)(2,1)S(1)}, bf16[2048,1536]{1,0:T(8,128)(2,1)S(1)}, u32[]{:S(2)}, u32[]{:S(2)}) collective-permute-start(bf16[2048,1536]{1,0:T(8,128)(2,1)S(1)} %get-tuple-element.24), channel_id=1, source_target_pairs={{0,2},{2,4},{4,6},{1,3},{3,5},{5,7}} | collective-permute-start | bytes 18874376 | tf_op jit(solution)/shard_map/ppermute | solution.py:43
  1908.6 144.8 %reduce-scatter.31.cloned.1.call-start = ((), (), s32[]{:S(2)}) async-start(), calls=%async_computation.31 | async-start | bytes 18874368 | tf_op jit(solution)/shard_map/reduce_scatter | solution.py:20
  2036.2 62.4 %all-gather.33.cloned.1.call-start = ((), (), s32[]{:S(2)}) async-start(), calls=%async_computation.32 | async-start | bytes 18874368 | tf_op jit(solution)/shard_map/all_gather | solution.py:17
  2074.5 143.8 %reduce-scatter.33.cloned.1.call-start = ((), (), s32[]{:S(2)}) async-start(), calls=%async_computation.33 | async-start | bytes 18874368 | tf_op jit(solution)/shard_map/reduce_scatter | solution.py:20
  2201.1 203.4 %all-gather.35.cloned.1.call-start = ((), (), s32[]{:S(2)}) async-start(), calls=%async_computation.34 | async-start | bytes 18874368 | tf_op jit(solution)/shard_map/all_gather | solution.py:17
  2229.1 138.9 %collective-permute-start.4 = (bf16[2048,1536]{1,0:T(8,128)(2,1)S(1)}, bf16[2048,1536]{1,0:T(8,128)(2,1)S(1)}, u32[]{:S(2)}, u32[]{:S(2)}) collective-permute-start(bf16[2048,1536]{1,0:T(8,128)(2,1)S(1)} %get-tuple-element.18), channel_id=1, source_target_pairs={{0,2},{2,4},{4,6},{1,3},{3,5},{5,7}} | collective-permute-start | bytes 18874376 | tf_op jit(solution)/shard_map/ppermute | solution.py:43
  2379.3 144.9 %reduce-scatter.35.cloned.1.call-start = ((), (), s32[]{:S(2)}) async-start(), calls=%async_computation.35 | async-start | bytes 18874368 | tf_op jit(solution)/shard_map/reduce_scatter | solution.py:20
  2507.1 62.4 %all-gather.37.cloned.1.call-start = ((), (), s32[]{:S(2)}) async-start(), calls=%async_computation.36 | async-start | bytes 18874368 | tf_op jit(solution)/shard_map/all_gather | solution.py:17
  2545.4 143.8 %reduce-scatter.37.cloned.1.call-start = ((), (), s32[]{:S(2)}) async-start(), calls=%async_computation.37 | async-start | bytes 18874368 | tf_op jit(solution)/shard_map/reduce_scatter | solution.py:20
  2672.0 203.4 %all-gather.39.cloned.1.call-start = ((), (), s32[]{:S(2)}) async-start(), calls=%async_computation.38 | async-start | bytes 18874368 | tf_op jit(solution)/shard_map/all_gather | solution.py:17
  2700.0 138.9 %collective-permute-start.5 = (bf16[2048,1536]{1,0:T(8,128)(2,1)S(1)}, bf16[2048,1536]{1,0:T(8,128)(2,1)S(1)}, u32[]{:S(2)}, u32[]{:S(2)}) collective-permute-start(bf16[2048,1536]{1,0:T(8,128)(2,1)S(1)} %get-tuple-element.12), channel_id=1, source_target_pairs={{0,2},{2,4},{4,6},{1,3},{3,5},{5,7}} | collective-permute-start | bytes 18874376 | tf_op jit(solution)/shard_map/ppermute | solution.py:43
  2850.2 144.9 %reduce-scatter.39.cloned.1.call-start = ((), (), s32[]{:S(2)}) async-start(), calls=%async_computation.39 | async-start | bytes 18874368 | tf_op jit(solution)/shard_map/reduce_scatter | solution.py:20
  2978.0 62.4 %all-gather.41.cloned.1.call-start = ((), (), s32[]{:S(2)}) async-start(), calls=%async_computation.40 | async-start | bytes 18874368 | tf_op jit(solution)/shard_map/all_gather | solution.py:17
  3016.3 147.1 %reduce-scatter.41.cloned.1.call-start = ((), (), s32[]{:S(2)}) async-start(), calls=%async_computation.41 | async-start | bytes 18874368 | tf_op jit(solution)/shard_map/reduce_scatter | solution.py:20
  (24 other events, 1212.6 us)
Sparse Core Ops, SparseCore 0:
  24.6 24.4 all-gather.14
  151.7 17.0 reduce-scatter.14
  182.0 23.9 all-gather.16
  308.6 17.0 reduce-scatter.16
  496.1 25.0 all-gather.18
  623.8 16.9 reduce-scatter.18
  662.0 23.9 all-gather.20
  788.7 17.0 reduce-scatter.20
  966.9 25.0 all-gather.22
  1094.6 16.9 reduce-scatter.22
  1132.9 23.9 all-gather.24
  1259.5 17.0 reduce-scatter.24
  1437.8 25.0 all-gather.26
  1565.5 16.9 reduce-scatter.26
  1603.8 23.9 all-gather.28
  1730.4 17.0 reduce-scatter.28
  1908.7 24.9 all-gather.30
  2036.3 16.9 reduce-scatter.30
  2074.6 23.9 all-gather.32
  2201.3 17.0 reduce-scatter.32
  2379.5 25.0 all-gather.34
  2507.2 17.0 reduce-scatter.34
  2545.5 23.9 all-gather.36
  2672.1 16.9 reduce-scatter.36
  2850.3 25.0 all-gather.38
  2978.1 16.9 reduce-scatter.38
  3016.4 23.9 all-gather.40
  3143.0 17.0 reduce-scatter.40
where the time goes:
time: 3190 us; the launch traced here: 3180 us
  matrix products  1430 us (45%)
  waiting for transfers between devices  1360 us (43%)
  other arithmetic  296 us (9%)
  local copies, waits for them, and re-layouts  64.6 us (2%)
    ppermute x6, waiting for transfers between devices, local(): recv = lax.ppermute(y, 'stage', fwd)  824 us
    dot_general x14, matrix products, _block(): jnp.dot(h, w1, preferred_element_type=jnp.float32)  780 us
    dot_general x14, matrix products, _block(): p = jnp.dot(a, w2, preferred_element_type=jnp.float32).astype(jnp.bfloat16)  654 us
    all_gather x14, waiting for transfers between devices, _block(): h = lax.all_gather(_ln(y, g), 'tp', axis=0, tiled=True)  344 us
    reduce_scatter x14, waiting for transfers between devices, _block(): r = lax.psum_scatter(p, 'tp', scatter_dimension=0, tiled=True)  191 us
    reduce_sum x14, other arithmetic, _ln(): mu = jnp.mean(yf, axis=-1, keepdims=True)  92.2 us
    convert_element_type x14, other arithmetic, _ln(): ((yf - mu) * lax.rsqrt(var + EPS) * g.astype(jnp.float32)).astype(jnp.bfl...  81.2 us
    dynamic_update_slice x7, other arithmetic, local(): lax.dynamic_update_index_in_dim(out, jnp.where((m >= 0) & (m < M), y, old...  77.1 us
  transfers between devices with their start and end apart: 34, of which 33 were waited for; matrix products, arithmetic and copies ran while one was open for 2% of the time, Pallas kernels for 0%

commit v1 on v0

v1 whole, which is shorter than its diff:
```python
import functools

import jax
import jax.numpy as jnp
from jax import lax
from jax.experimental import pallas as pl
from jax.experimental.pallas import tpu as pltpu
from jax.sharding import PartitionSpec as P

EPS = 1e-5
EXPLICIT = False
C = 128
NS = 8
NO = 4
F1K = 18
T = 256


def _gelu(u):
    k0 = 0.7978845608028654
    k1 = k0 * 0.044715
    return u * (0.5 + 0.5 * jnp.tanh(u * (k0 + k1 * (u * u))))


def _kernel(S, M, TL, D, FH, x, g, w1, w2, y,
            w1v, w2v, gv, gf, ybuf, ob, h, a,
            rs, ss, osem, yr, xs, wl, wrs, wrr, gs, credit):
    KT, NH = D // T, FH // T
    NT = 2 * NH
    NP, N2 = NT // 2, KT // 2
    CPM = TL // C
    HC = M * CPM
    NC = 2 * HC
    LX = NS - 2

    p = lax.axis_index('stage')
    i = lax.axis_index('tp')
    j = 2 * p + i
    last = 2 * S - 1
    has_prev, has_next = j > 0, j < last
    odd = i == 1
    prv = (lax.rem(p + S - 1 + i, S), 1 - i)
    nxt = (lax.rem(p + i, S), 1 - i)
    partner = (p, 1 - i)
    MESH = pl.DeviceIdType.MESH

    def tok(ref, q):
        q = lax.rem(q, HC)
        return ref.at[lax.div(q, CPM), pl.ds(pl.multiple_of(lax.rem(q, CPM) * C, C), C), :]

    def arrival(q):
        s = lax.rem(q, NS)
        return pltpu.make_async_copy(tok(x, q), ybuf.at[s], rs.at[s])

    def send(q):
        so, s = lax.rem(q, NO), lax.rem(q, NS)
        return pltpu.make_async_remote_copy(ob.at[so], ybuf.at[s], ss.at[so], rs.at[s], device_id=nxt, device_id_type=MESH)

    def out_local(q):
        so = lax.rem(q, NO)
        return pltpu.make_async_copy(ob.at[so], tok(y.at[0], q), osem.at[so])

    def out_remote(q):
        so = lax.rem(q, NO)
        return pltpu.make_async_remote_copy(ob.at[so], tok(y.at[0], q), osem.at[so], yr.at[0], device_id=partner, device_id_type=MESH)

    def xpush(q):
        s = lax.rem(q, NS)
        return pltpu.make_async_remote_copy(tok(x, q), ybuf.at[s], xs.at[0], rs.at[s], device_id=prv, device_id_type=MESH)

    local1 = [pltpu.make_async_copy(w1.at[0, i, :, pl.ds(n * T, T)], w1v.at[n], wl.at[0]) for n in range(NH)]
    local2 = [pltpu.make_async_copy(w2.at[0, i, :, pl.ds(n * T, T)], w2v.at[n, pl.ds(0, FH), :], wl.at[1]) for n in range(KT)]
    remote1 = [pltpu.make_async_remote_copy(w1.at[0, 1 - i, :, pl.ds(n * T, T)], w1v.at[NH + n], wrs.at[0], wrr.at[0],
                                            device_id=partner, device_id_type=MESH) for n in range(NH)]
    remote2 = [pltpu.make_async_remote_copy(w2.at[0, 1 - i, :, pl.ds(n * T, T)], w2v.at[n, pl.ds(FH, FH), :], wrs.at[1], wrr.at[1],
                                            device_id=partner, device_id_type=MESH) for n in range(KT)]
    whole1, whole2 = w1v.at[pl.ds(0, NH)], w2v.at[:, pl.ds(0, FH), :]
    own1, got1, sent1 = (pltpu.make_async_copy(whole1, whole1, sem) for sem in (wl.at[0], wrr.at[0], wrs.at[0]))
    own2, got2, sent2 = (pltpu.make_async_copy(whole2, whole2, sem) for sem in (wl.at[1], wrr.at[1], wrs.at[1]))
    gcopy = pltpu.make_async_copy(g.at[0], gv, gs.at[0])

    bar = pltpu.get_barrier_semaphore()

    @pl.when(has_prev)
    def _():
        pl.semaphore_signal(bar, 1, device_id=prv, device_id_type=MESH)

    @pl.when(has_next)
    def _():
        pl.semaphore_signal(bar, 1, device_id=nxt, device_id_type=MESH)

    gcopy.start()

    @pl.when(j == 0)
    def _():
        for q in range(NS - 1):
            arrival(q).start()

    for cp in local1:
        cp.start()

    @pl.when(has_prev & has_next)
    def _():
        pl.semaphore_wait(bar, 2)

    @pl.when((j == 0) | (j == last))
    def _():
        pl.semaphore_wait(bar, 1)

    for cp in remote1:
        cp.start()
    for cp in local2:
        cp.start()
    for cp in remote2:
        cp.start()

    @pl.when(has_prev)
    def _():
        pl.semaphore_signal(credit, NS, device_id=prv, device_id_type=MESH)

    gcopy.wait()
    gf[...] = jnp.where(odd, gv[1:2, :].astype(jnp.float32), gv[0:1, :].astype(jnp.float32))

    def ln(s):
        for r in range(0, C, 64):
            yf = ybuf[s, r:r + 64, :].astype(jnp.float32)
            mu = jnp.mean(yf, axis=-1, keepdims=True)
            d = yf - mu
            var = jnp.mean(jnp.square(d), axis=-1, keepdims=True)
            hh = (d * lax.rsqrt(var + EPS) * gf[...]).astype(jnp.bfloat16)
            for k in range(KT):
                h[k, r:r + 64, :] = hh[:, k * T:(k + 1) * T]

    def take_in(q):
        arrival(q + 1).wait()

    def slot_free(q):
        @pl.when(has_next)
        def _():
            send(q).wait_send()

        @pl.when(odd)
        def _():
            out_local(q).wait()

    def put_out(q):
        @pl.when(has_next)
        def _():
            pl.semaphore_wait(credit, 1)
            send(q).start()

        @pl.when(odd & (q < HC))
        def _():
            out_remote(q).start()

        @pl.when(odd & (q >= HC))
        def _():
            out_local(q).start()

        @pl.when(has_prev)
        def _():
            pl.semaphore_signal(credit, 1, device_id=prv, device_id_type=MESH)

        @pl.when((j == 0) & (q + NS - 1 < HC))
        def _():
            arrival(q + NS - 1).start()

        @pl.when((j == 1) & (q + LX >= HC) & (q + LX < NC))
        def _():
            @pl.when(q + LX > HC)
            def _():
                xpush(q + LX - 1).wait_send()
            xpush(q + LX).start()

    items2 = [(2, k, n) for k in range(NT) for n in range(N2)]
    items1 = [(1, k, n) for n in range(NP) for k in range(KT)]

    def res_store(q, col, t):
        s, so = lax.rem(q, NS), lax.rem(q, NO)
        ob[so, :, col:col + T] = (ybuf[s, :, col:col + T].astype(jnp.float32) + t).astype(jnp.bfloat16)

    def main(*accs):
        A = (accs[:8], accs[8:])
        acc1 = lambda n: N2 + n % (8 - N2)

        def push(it, reg):
            ty, k, n = it
            for u in range(2):
                w = (w1v if ty == 1 else w2v)[2 * n + u, k * T:(k + 1) * T, :]
                pltpu.matmul_push_rhs(w, staging_register=reg, mxu_index=u)

        def acc(it, reg):
            ty, k, n = it
            lhs = (h if ty == 1 else a)[k]
            for u in range(2):
                pltpu.matmul_acc_lhs(A[u][acc1(n) if ty == 1 else n], lhs, load_staged_rhs=reg)

        def pop1(n):
            if EXPLICIT:
                t = [pltpu.matmul_pop(A[u][acc1(n)]) for u in range(2)]
            else:
                lhs = jnp.concatenate([h[k] for k in range(KT)], axis=1)
                rhs = jnp.concatenate([w1v[2 * n], w1v[2 * n + 1]], axis=1)
                t = jnp.dot(lhs, rhs, preferred_element_type=jnp.float32)
                t = [t[:, :T], t[:, T:]]
            for u in range(2):
                a[2 * n + u] = _gelu(t[u]).astype(jnp.bfloat16)

        def pop2(q, n):
            if EXPLICIT:
                t = [pltpu.matmul_pop(A[u][n]) for u in range(2)]
            else:
                lhs = jnp.concatenate([a[k] for k in range(NT)], axis=1)
                rhs = jnp.concatenate([w2v[2 * n], w2v[2 * n + 1]], axis=1)
                t = jnp.dot(lhs, rhs, preferred_element_type=jnp.float32)
                t = [t[:, :T], t[:, T:]]
            for u in range(2):
                res_store(q, (2 * n + u) * T, t[u])

        def run(items, reg0, hooks, following):
            for idx, it in enumerate(items):
                reg = (reg0 + idx) % 2
                nx = items[idx + 1] if idx + 1 < len(items) else following
                if EXPLICIT:
                    if nx is not None:
                        push(nx, 1 - reg)
                    acc(it, reg)
                if idx in hooks:
                    hooks[idx]()

        L2, L1 = len(items2), len(items1)

        arrival(0).wait()
        ln(0)
        own1.wait()
        hooks = {}
        for n in range(NP - 1):
            hooks[(n + 2) * KT - 1] = functools.partial(pop1, n)

        half = NP // 2
        hooks[half * KT - 2] = got1.wait
        hooks[L1 - 2] = lambda: (own2.wait(), got2.wait())
        if EXPLICIT:
            push(items1[0], 0)
        run(items1, 0, hooks, items2[0])

        def body(q, _):
            def f1():
                take_in(q)

                @pl.when(q >= NO)
                def _():
                    slot_free(q - NO)
                ln(lax.rem(q + 1, NS))

            def f2():
                for n in range(N2):
                    pop2(q, n)
                put_out(q)
            hk = {N2 * 4 - 1: functools.partial(pop1, NP - 1), F1K * N2 - 1: f1, L2 + KT - 1: f2}
            for n in range(NP - 1):
                hk[L2 + (n + 2) * KT - 1] = functools.partial(pop1, n)
            run(items2 + items1, 0, hk, items2[0])
            return 0

        lax.fori_loop(0, NC - 1, body, 0)

        q = jnp.int32(NC - 1)
        slot_free(q - NO)
        run(items2, 0, {N2 * 4 - 1: functools.partial(pop1, NP - 1)}, None)
        for n in range(N2):
            pop2(q, n)
        put_out(q)

    if EXPLICIT:
        pl.run_scoped(main, *([pltpu.ACC(0)((C, T), jnp.float32)] * 8 + [pltpu.ACC(1)((C, T), jnp.float32)] * 8))
    else:
        main(*([None] * 16))

    for d in range(NO):
        slot_free(jnp.int32(NC - NO + d))

    @pl.when(has_next)
    def _():
        pl.semaphore_wait(credit, NS)

    @pl.when(j == 1)
    def _():
        xpush(jnp.int32(NC - 1)).wait_send()

    sent1.wait()
    sent2.wait()

    @pl.when(i == 0)
    def _():
        pltpu.make_async_copy(y, y, yr.at[0]).wait()


def solution(mesh):
    S = mesh.shape['stage']

    def local(x, g, w1, w2):
        M, TL, D = x.shape
        FH = w1.shape[-1]
        bf = jnp.bfloat16
        dma = pltpu.SemaphoreType.DMA
        flops = 4 * M * 2 * TL * D * 2 * FH
        return pl.pallas_call(
            functools.partial(_kernel, S, M, TL, D, FH),
            out_shape=jax.ShapeDtypeStruct((1, M, TL, D), bf),
            in_specs=[pl.BlockSpec(memory_space=pl.ANY)] * 4,
            out_specs=pl.BlockSpec(memory_space=pl.ANY),
            scratch_shapes=[
                pltpu.VMEM((2 * FH // T, D, T), bf),
                pltpu.VMEM((D // T, 2 * FH, T), bf),
                pltpu.VMEM((2, D), bf),
                pltpu.VMEM((1, D), jnp.float32),
                pltpu.VMEM((NS, C, D), bf),
                pltpu.VMEM((NO, C, D), bf),
                pltpu.VMEM((D // T, C, T), bf),
                pltpu.VMEM((2 * FH // T, C, T), bf),
                dma((NS,)), dma((NO,)), dma((NO,)), dma((1,)), dma((1,)),
                dma((2,)), dma((2,)), dma((2,)), dma((1,)),
                pltpu.SemaphoreType.REGULAR,
            ],
            compiler_params=pltpu.CompilerParams(
                collective_id=0, has_side_effects=True, vmem_limit_bytes=67043328),
            cost_estimate=pl.CostEstimate(flops=flops, bytes_accessed=4 * M * TL * D, transcendentals=0),
        )(x, g, w1, w2)

    return jax.shard_map(
        local, mesh=mesh,
        in_specs=(P(None, 'tp', None), P('stage', None, None),
                  P('stage', None, None, 'tp'), P('stage', None, 'tp', None)),
        out_specs=P('stage', None, 'tp', None), check_vma=False)
```

time: 3190 us -> 847 us (0.27)
  matrix products: 1430 us -> 0 us
  waiting for transfers between devices: 1360 us -> 0 us
  Pallas kernels: 0 us -> 827 us
  other arithmetic: 296 us -> 0 us
  local copies, waits for them, and re-layouts: 64.6 us -> 20.5 us
    dot_general x28 -> x0, matrix products: 1430 us -> none  [the longest x14 780 us: _block(): jnp.dot(h, w1, preferred_element_type=jnp.float32)]
    pallas_call x0 -> x1, Pallas kernels: none -> 827 us  [local(): pl.pallas_call(functools.partial(_kernel, S, M, TL, D, FH), out_shape=jax...]
    ppermute x6 -> x0, waiting for transfers between devices: 824 us -> none  [local(): recv = lax.ppermute(y, 'stage', fwd)]
    all_gather x14 -> x0, waiting for transfers between devices: 344 us -> none  [_block(): h = lax.all_gather(_ln(y, g), 'tp', axis=0, tiled=True)]
    reduce_scatter x14 -> x0, waiting for transfers between devices: 191 us -> none  [_block(): r = lax.psum_scatter(p, 'tp', scatter_dimension=0, tiled=True)]
    reduce_sum x28 -> x0, other arithmetic: 137 us -> none  [the longest x14 92.2 us: _ln(): mu = jnp.mean(yf, axis=-1, keepdims=True)]
    convert_element_type x15 -> x0, other arithmetic: 81.9 us -> none  [the longest x14 81.2 us: _ln(): ((yf - mu) * lax.rsqrt(var + EPS) * g.astype(jnp.float32)).astype(jnp.bfl...]
    dynamic_update_slice x7 -> x0, other arithmetic: 77.1 us -> none  [local(): lax.dynamic_update_index_in_dim(out, jnp.where((m >= 0) & (m < M), y, old...]
  transfers between devices with their start and end apart: 34 -> 0, of which waited for: 33 -> 0; matrix products, arithmetic and copies ran while one was open for 2% -> 0% of each run, Pallas kernels for 0% -> 0%
where the time goes in v1:
time: 847 us
  Pallas kernels  827 us (98%)
  local copies, waits for them, and re-layouts  20.5 us (2%)
    pallas_call x1, Pallas kernels, local(): pl.pallas_call(functools.partial(_kernel, S, M, TL, D, FH), out_shape=jax...  827 us
    unnamed x1, local copies, waits for them, and re-layouts  20.5 us

profile of v1, /device:TPU:7, one launch (start us, length us, event | category | flops | bytes accessed | tf_op | source)
XLA Modules:
  0.0 847.0 jit_solution(9708839854824444005)
XLA Ops:
  0.0 826.5 %shard_map.46 = bf16[1,4,2048,1536]{3,2,1,0:T(8,128)(2,1)} custom-call(bf16[4,2048,1536]{2,1,0:T(8,128)(2,1)} %x.1, bf16[1,2,1536]{2,1,0:T(2,128)(2,1)} %g.1, bf16[1,2,1536,3072]{3,2,1,0:T(8,128)(2,1)} %w1.1, bf16[1,2,3072,1536]{3,2,1,0:T(8,128)(2,1)} %w2.1), custom_call_target="tpu_custom_call" | custom-call | flops 618475290624 | bytes 50331648 | tf_op jit(solution)/shard_map/pallas_call | solution.py:308
  826.5 20.5 %copy.6 = bf16[1,4,2048,1536]{3,2,1,0:T(8,128)(2,1)} copy(bf16[1,4,2048,1536]{3,2,1,0:T(8,128)(2,1)} %shard_map.46) | data formatting | bytes 50331648

commit v2 on v0

v2 whole, which is shorter than its diff:
```python
import functools

import jax
import jax.numpy as jnp
from jax import lax
from jax.experimental import pallas as pl
from jax.experimental.pallas import tpu as pltpu
from jax.sharding import PartitionSpec as P

EPS = 1e-5
C = 144
NS = 8
NO = 4
T = 256


def _gelu(u):
    k0 = 0.7978845608028654
    k1 = k0 * 0.044715
    return u * (0.5 + 0.5 * jnp.tanh(u * (k0 + k1 * (u * u))))


def _kernel(S, R, D, FH, x, g, w1, w2, y,
            w1v, w2v, gv, gf, ybuf, ob, h, a,
            rs, ss, osem, otail, yr, xs, wl, wrs, wrr, gs, credit):
    KT, NH = D // T, FH // T
    NT = 2 * NH
    NP, N2 = NT // 2, KT // 2
    HC = -(-R // C)
    OV = HC * C - R
    NC = 2 * HC
    LX = NS - 2
    B = C - OV

    p = lax.axis_index('stage')
    i = lax.axis_index('tp')
    j = 2 * p + i
    last = 2 * S - 1
    has_next = j < last
    odd = i == 1
    prv = (lax.rem(p + S - 1 + i, S), 1 - i)
    nxt = (lax.rem(p + i, S), 1 - i)
    partner = (p, 1 - i)
    MESH = pl.DeviceIdType.MESH

    def rows(q, skip=0, n=C):
        r = lax.rem(q, HC)
        at = r * C - lax.div(r, HC - 1) * OV + skip
        return pl.ds(pl.multiple_of(at, 16), n)

    def arrival(q):
        s = lax.rem(q, NS)
        return pltpu.make_async_copy(x.at[rows(q), :], ybuf.at[s], rs.at[s])

    def send(q):
        so, s = lax.rem(q, NO), lax.rem(q, NS)
        return pltpu.make_async_remote_copy(ob.at[so], ybuf.at[s], ss.at[so], rs.at[s], device_id=nxt, device_id_type=MESH)

    def xpush(q):
        s = lax.rem(q, NS)
        return pltpu.make_async_remote_copy(x.at[rows(q), :], ybuf.at[s], xs.at[0], rs.at[s], device_id=prv, device_id_type=MESH)

    def out_local(q):
        so = lax.rem(q, NO)
        return pltpu.make_async_copy(ob.at[so, pl.ds(OV, B)], y.at[rows(q, OV, B), :], osem.at[so])

    def out_remote(q):
        so = lax.rem(q, NO)
        return pltpu.make_async_remote_copy(ob.at[so, pl.ds(OV, B)], y.at[rows(q, OV, B), :], osem.at[so], yr.at[0],
                                            device_id=partner, device_id_type=MESH)

    def tail_local(q):
        so = lax.rem(q, NO)
        return pltpu.make_async_copy(ob.at[so, pl.ds(0, OV)], y.at[rows(q, 0, OV), :], otail.at[so])

    def tail_remote(q):
        so = lax.rem(q, NO)
        return pltpu.make_async_remote_copy(ob.at[so, pl.ds(0, OV)], y.at[rows(q, 0, OV), :], otail.at[so], yr.at[0],
                                            device_id=partner, device_id_type=MESH)

    def whole(q):
        return lax.rem(q, HC) < HC - 1

    local1 = [pltpu.make_async_copy(w1.at[0, i, :, pl.ds(n * T, T)], w1v.at[n], wl.at[0]) for n in range(NH)]
    local2 = [pltpu.make_async_copy(w2.at[0, i, :, pl.ds(n * T, T)], w2v.at[n, pl.ds(0, FH), :], wl.at[1]) for n in range(KT)]
    remote1 = [pltpu.make_async_remote_copy(w1.at[0, 1 - i, :, pl.ds(n * T, T)], w1v.at[NH + n], wrs.at[0], wrr.at[0],
                                            device_id=partner, device_id_type=MESH) for n in range(NH)]
    remote2 = [pltpu.make_async_remote_copy(w2.at[0, 1 - i, :, pl.ds(n * T, T)], w2v.at[n, pl.ds(FH, FH), :], wrs.at[1], wrr.at[1],
                                            device_id=partner, device_id_type=MESH) for n in range(KT)]
    half1, half2 = w1v.at[pl.ds(0, NH)], w2v.at[:, pl.ds(0, FH), :]
    own1, got1, sent1 = (pltpu.make_async_copy(half1, half1, sem) for sem in (wl.at[0], wrr.at[0], wrs.at[0]))
    own2, got2, sent2 = (pltpu.make_async_copy(half2, half2, sem) for sem in (wl.at[1], wrr.at[1], wrs.at[1]))
    gcopy = pltpu.make_async_copy(g.at[0], gv, gs.at[0])

    bar = pltpu.get_barrier_semaphore()

    pl.semaphore_signal(bar, 1, device_id=prv, device_id_type=MESH)
    pl.semaphore_signal(bar, 1, device_id=nxt, device_id_type=MESH)
    gcopy.start()

    @pl.when(j == 0)
    def _():
        for q in range(NS - 1):
            arrival(q).start()

    for cp in local1:
        cp.start()

    pl.semaphore_wait(bar, 2)
    for cp in remote1:
        cp.start()
    for cp in local2:
        cp.start()
    for cp in remote2:
        cp.start()

    pl.semaphore_signal(credit, NS, device_id=prv, device_id_type=MESH)

    gcopy.wait()
    gf[...] = jnp.where(odd, gv[1:2, :].astype(jnp.float32), gv[0:1, :].astype(jnp.float32))

    def ln(s):
        for r in range(0, C, 48):
            yf = ybuf[s, r:r + 48, :].astype(jnp.float32)
            mu = jnp.mean(yf, axis=-1, keepdims=True)
            d = yf - mu
            var = jnp.mean(jnp.square(d), axis=-1, keepdims=True)
            hh = (d * lax.rsqrt(var + EPS) * gf[...]).astype(jnp.bfloat16)
            for k in range(KT):
                h[k, r:r + 48, :] = hh[:, k * T:(k + 1) * T]

    def mm1(n):
        lhs = jnp.concatenate([h[k] for k in range(KT)], axis=1)
        rhs = jnp.concatenate([w1v[2 * n], w1v[2 * n + 1]], axis=1)
        t = jnp.dot(lhs, rhs, preferred_element_type=jnp.float32)
        for u in range(2):
            a[2 * n + u] = _gelu(t[:, u * T:(u + 1) * T]).astype(jnp.bfloat16)

    def mm2(n, q):
        s, so = lax.rem(q, NS), lax.rem(q, NO)
        lhs = jnp.concatenate([a[k] for k in range(NT)], axis=1)
        rhs = jnp.concatenate([w2v[2 * n], w2v[2 * n + 1]], axis=1)
        t = jnp.dot(lhs, rhs, preferred_element_type=jnp.float32)
        cols = slice(2 * n * T, 2 * (n + 1) * T)
        ob[so, :, cols] = (ybuf[s, :, cols].astype(jnp.float32) + t).astype(jnp.bfloat16)

    def slot_free(q):
        @pl.when(has_next)
        def _():
            send(q).wait_send()

        @pl.when(odd)
        def _():
            out_local(q).wait()

        if OV:
            @pl.when(odd & whole(q))
            def _():
                tail_local(q).wait()

    def put_out(q):
        pl.semaphore_wait(credit, 1)
        pl.semaphore_signal(credit, 1, device_id=prv, device_id_type=MESH)

        @pl.when(has_next)
        def _():
            send(q).start()

        @pl.when(odd & (q < HC))
        def _():
            out_remote(q).start()

        @pl.when(odd & (q >= HC))
        def _():
            out_local(q).start()

        if OV:
            @pl.when(odd & (q < HC) & whole(q))
            def _():
                tail_remote(q).start()

            @pl.when(odd & (q >= HC) & whole(q))
            def _():
                tail_local(q).start()

        @pl.when((j == 0) & (q + NS - 1 < HC))
        def _():
            arrival(q + NS - 1).start()

        @pl.when((j == 1) & (q + LX > HC) & (q + LX < NC))
        def _():
            xpush(q + LX - 1).wait_send()

        @pl.when((j == 1) & (q + LX >= HC) & (q + LX < NC))
        def _():
            xpush(q + LX).start()

    arrival(0).wait()
    ln(0)

    def body(q, first):
        for n in range(NP):
            if first and n == 0:
                own1.wait()
            if first and n == NP // 2:
                got1.wait()
            mm1(n)
        if first:
            own2.wait()
            got2.wait()
        for n in range(N2 - 1):
            mm2(n, q)

        @pl.when(q + 1 < NC)
        def _():
            arrival(q + 1).wait()
        ln(lax.rem(q + 1, NS))
        mm2(N2 - 1, q)
        put_out(q)

        @pl.when(q + 1 >= NO)
        def _():
            slot_free(q + 1 - NO)
        return 0

    body(jnp.int32(0), True)
    lax.fori_loop(1, NC, lambda q, _: body(q, False), 0)

    for d in range(1, NO):
        slot_free(jnp.int32(NC - NO + d))

    pl.semaphore_wait(credit, NS)

    @pl.when(j == 1)
    def _():
        xpush(jnp.int32(NC - 1)).wait_send()

    sent1.wait()
    sent2.wait()

    @pl.when(i == 0)
    def _():
        pltpu.make_async_copy(y, y, yr.at[0]).wait()


def solution(mesh):
    S = mesh.shape['stage']

    def local(x, g, w1, w2):
        M, TL, D = x.shape
        FH = w1.shape[-1]
        bf = jnp.bfloat16
        dma = pltpu.SemaphoreType.DMA
        out = pl.pallas_call(
            functools.partial(_kernel, S, M * TL, D, FH),
            out_shape=jax.ShapeDtypeStruct((M * TL, D), bf),
            in_specs=[pl.BlockSpec(memory_space=pl.ANY)] * 4,
            out_specs=pl.BlockSpec(memory_space=pl.ANY),
            scratch_shapes=[
                pltpu.VMEM((2 * FH // T, D, T), bf),
                pltpu.VMEM((D // T, 2 * FH, T), bf),
                pltpu.VMEM((2, D), bf),
                pltpu.VMEM((1, D), jnp.float32),
                pltpu.VMEM((NS, C, D), bf),
                pltpu.VMEM((NO, C, D), bf),
                pltpu.VMEM((D // T, C, T), bf),
                pltpu.VMEM((2 * FH // T, C, T), bf),
                dma((NS,)), dma((NO,)), dma((NO,)), dma((NO,)), dma((1,)), dma((1,)),
                dma((2,)), dma((2,)), dma((2,)), dma((1,)),
                pltpu.SemaphoreType.REGULAR,
            ],
            compiler_params=pltpu.CompilerParams(
                collective_id=0, has_side_effects=True, vmem_limit_bytes=67043328),
            cost_estimate=pl.CostEstimate(flops=8 * M * TL * D * 2 * FH, bytes_accessed=4 * M * TL * D, transcendentals=0),
        )(x.reshape(M * TL, D), g, w1, w2)
        return out.reshape(1, M, TL, D)

    return jax.shard_map(
        local, mesh=mesh,
        in_specs=(P(None, 'tp', None), P('stage', None, None),
                  P('stage', None, None, 'tp'), P('stage', None, 'tp', None)),
        out_specs=P('stage', None, 'tp', None), check_vma=False)
```

time: 3190 us -> 805 us (0.25)
  matrix products: 1430 us -> 0 us
  waiting for transfers between devices: 1360 us -> 0 us
  Pallas kernels: 0 us -> 784 us
  other arithmetic: 296 us -> 0 us
  local copies, waits for them, and re-layouts: 64.6 us -> 20.5 us
    dot_general x28 -> x0, matrix products: 1430 us -> none  [the longest x14 780 us: _block(): jnp.dot(h, w1, preferred_element_type=jnp.float32)]
    ppermute x6 -> x0, waiting for transfers between devices: 824 us -> none  [local(): recv = lax.ppermute(y, 'stage', fwd)]
    pallas_call x0 -> x1, Pallas kernels: none -> 784 us  [local(): pl.pallas_call(functools.partial(_kernel, S, M * TL, D, FH), out_shape=ja...]
    all_gather x14 -> x0, waiting for transfers between devices: 344 us -> none  [_block(): h = lax.all_gather(_ln(y, g), 'tp', axis=0, tiled=True)]
    reduce_scatter x14 -> x0, waiting for transfers between devices: 191 us -> none  [_block(): r = lax.psum_scatter(p, 'tp', scatter_dimension=0, tiled=True)]
    reduce_sum x28 -> x0, other arithmetic: 137 us -> none  [the longest x14 92.2 us: _ln(): mu = jnp.mean(yf, axis=-1, keepdims=True)]
    convert_element_type x15 -> x0, other arithmetic: 81.9 us -> none  [the longest x14 81.2 us: _ln(): ((yf - mu) * lax.rsqrt(var + EPS) * g.astype(jnp.float32)).astype(jnp.bfl...]
    dynamic_update_slice x7 -> x0, other arithmetic: 77.1 us -> none  [local(): lax.dynamic_update_index_in_dim(out, jnp.where((m >= 0) & (m < M), y, old...]
  transfers between devices with their start and end apart: 34 -> 0, of which waited for: 33 -> 0; matrix products, arithmetic and copies ran while one was open for 2% -> 0% of each run, Pallas kernels for 0% -> 0%
where the time goes in v2:
time: 805 us
  Pallas kernels  784 us (97%)
  local copies, waits for them, and re-layouts  20.5 us (3%)
    pallas_call x1, Pallas kernels, local(): pl.pallas_call(functools.partial(_kernel, S, M * TL, D, FH), out_shape=ja...  784 us
    unnamed x1, local copies, waits for them, and re-layouts  20.5 us

profile of v2, /device:TPU:7, one launch (start us, length us, event | category | flops | bytes accessed | tf_op | source)
XLA Modules:
  0.0 804.9 jit_solution(7878897092197389159)
XLA Ops:
  0.0 784.4 %shard_map.46 = bf16[8192,1536]{1,0:T(8,128)(2,1)} custom-call(bf16[8192,1536]{1,0:T(8,128)(2,1)} %bitcast.3, bf16[1,2,1536]{2,1,0:T(2,128)(2,1)} %g.1, bf16[1,2,1536,3072]{3,2,1,0:T(8,128)(2,1)} %w1.1, bf16[1,2,3072,1536]{3,2,1,0:T(8,128)(2,1)} %w2.1), custom_call_target="tpu_custom_call" | custom-call | flops 618475290624 | bytes 50331648 | tf_op jit(solution)/shard_map/pallas_call | solution.py:254
  784.4 20.5 %copy.6 = bf16[1,4,2048,1536]{3,2,1,0:T(8,128)(2,1)} copy(bf16[1,4,2048,1536]{3,2,1,0:T(8,128)(2,1)} %bitcast.2) | data formatting | bytes 50331648
